TPU v7x, 32 devices: a whole 2x2x4 slice. The times are simulated.
32 devices in a mesh: sub: 8 (over z, x), tile: 4 (over y, core).
Axes of the slice: x: 2, y: 2, z: 4, core: 2. Of those that a mesh axis runs over, the one named last changes fastest.
Arguments:
- coupling: bfloat16 [8, 28, 256, 256], P('sub'), may hold values from -0.125 to 0.125
- panel_inv: float32 [8, 8, 256, 256], P('sub')
- a_ib: bfloat16 [8, 2048, 3072], P('sub', None, 'tile'), may hold values from -0.5 to 0.5
- owner: int32 [8, 12, 12], P('sub', None, 'tile'), may hold values from 0 to 7, as said below
- slot: int32 [8, 12, 12], P('sub', None, 'tile'), may hold values from 0 to 15
- base: bfloat16 [8, 64, 256, 256], P('sub', 'tile'), may hold values from -2 to 2
Outputs:
- assembled: bfloat16 [8, 64, 256, 256], P('sub', 'tile')
Inputs may be any that keep to these rules, and one draw needn't show every extreme that they name: `owner`: tiles of one device are those of one subdomain s and tile columns t*12/4 to (t+1)*12/4 - 1. At most 5 tiles of one device name one sub index; for each t one sub index, drawn from the seed, is named by exactly 5 tiles of every device of that t.
All inputs are finite; a program needn't handle non-finite values.
Results may differ from a plain program's by a relative error of at most 0.0051.
Values may be sent and summed in bfloat16 or wider, within the bound.
A program may use at most 128 MiB of HBM per device.

v0:
```python
import jax
import jax.numpy as jnp
from jax import lax
from jax.sharding import PartitionSpec as P


def solve(lower_blocks, inverse, right_cols):
    panel_width = inverse.shape[1]
    panels = []
    for row_panel in range(inverse.shape[0]):
        target = right_cols[row_panel * panel_width : (row_panel + 1) * panel_width].astype(
            jnp.float32
        )
        if row_panel > 0:
            block_start = row_panel * (row_panel - 1) // 2
            blocks = lower_blocks[block_start : block_start + row_panel]
            joined = jnp.transpose(blocks, (1, 0, 2)).reshape(panel_width, row_panel * panel_width)
            target = target - jnp.dot(
                joined, jnp.concatenate(panels, axis=0), preferred_element_type=jnp.float32
            )
        solved_panel = jnp.dot(
            inverse[row_panel],
            target,
            precision=lax.Precision.HIGHEST,
            preferred_element_type=jnp.float32,
        )
        panels.append(solved_panel.astype(jnp.bfloat16))
    return jnp.concatenate(panels, axis=0)


def inner_rows(left_part, right_part):
    return lax.dot_general(
        left_part, right_part, (((0,), (0,)), ((), ())), preferred_element_type=jnp.float32
    )


def shards(coupling, panel_inv, a_ib, owner, slot, base):
    lower_blocks = coupling[0]
    inverse = panel_inv[0]
    right_cols = a_ib[0]
    panel_width = inverse.shape[1]
    col_count = right_cols.shape[1]
    own_solved = solve(lower_blocks, inverse, right_cols)
    schur_cols = inner_rows(lax.all_gather(own_solved, "tile", axis=1, tiled=True), own_solved)
    tile_rows = schur_cols.shape[0] // panel_width
    col_tiles = col_count // panel_width
    tile_count = tile_rows * col_tiles
    contrib = (
        (-schur_cols).astype(jnp.bfloat16).reshape(tile_rows, panel_width, col_tiles, panel_width)
    )
    contrib = contrib.transpose(0, 2, 1, 3).reshape(tile_count, panel_width * panel_width)
    peer_count = lax.axis_size("sub")
    capacity = (tile_count + peer_count - 1) // peer_count
    owners_flat = owner[0].reshape(tile_count)
    slot_flat = slot[0].reshape(tile_count)
    position = jnp.arange(tile_count, dtype=jnp.int32)
    matching = owners_flat[:, None] == owners_flat[None, :]
    earlier = position[None, :] < position[:, None]
    ranking = jnp.sum(jnp.where(matching & earlier, 1, 0), axis=1).astype(jnp.int32)
    target = owners_flat * capacity + ranking
    seat_index = jnp.arange(peer_count * capacity, dtype=jnp.int32)
    selector = seat_index[:, None] == target[None, :]
    outgoing = jnp.dot(
        selector.astype(jnp.bfloat16), contrib, preferred_element_type=jnp.float32
    ).astype(jnp.bfloat16)
    outgoing = outgoing.reshape(peer_count, capacity, panel_width * panel_width)
    labels = jnp.sum(jnp.where(selector, slot_flat[None, :] + 1, 0), axis=1) - 1
    labels = labels.reshape(peer_count, capacity)
    incoming, landed = (
        lax.all_to_all(outgoing, "sub", split_axis=0, concat_axis=0, tiled=True),
        lax.all_to_all(labels, "sub", split_axis=0, concat_axis=0, tiled=True),
    )
    slots_here = base.shape[1]
    landing = (
        jnp.arange(slots_here, dtype=jnp.int32)[:, None]
        == landed.reshape(peer_count * capacity)[None, :]
    ).astype(jnp.bfloat16)
    summed = jnp.dot(
        landing,
        incoming.reshape(peer_count * capacity, panel_width * panel_width),
        preferred_element_type=jnp.float32,
    )
    result = (
        base[0].reshape(slots_here, panel_width * panel_width).astype(jnp.float32) + summed
    ).astype(jnp.bfloat16)
    return result.reshape(1, slots_here, panel_width, panel_width)


def solution(mesh):
    placed = (
        P("sub", None, None, None),
        P("sub", None, None, None),
        P("sub", None, "tile"),
        P("sub", None, "tile"),
        P("sub", None, "tile"),
        P("sub", "tile", None, None),
    )
    return jax.shard_map(
        shards, mesh=mesh, in_specs=placed, out_specs=P("sub", "tile", None, None), check_vma=False
    )
```

profile of v0, /device:TPU:0, one launch (start us, length us, event | category | flops | bytes accessed | tf_op | source)
XLA Modules:
  0.0 418.4 jit_solution(15891893024641498955)
XLA Ops:
  8.5 2.1 slice.121
  12.5 2.1 slice.129
  17.2 2.7 constant_dynamic-update-slice_fusion.17
  30.4 2.1 copy.61
  33.4 2.2 copy.63
  35.7 2.0 copy.64
  37.7 2.3 copy.65
  41.9 2.2 copy.67
  45.6 3.0 constant_dynamic-update-slice_fusion.16
  65.6 7.3 %all-to-all-start = ((s32[8,1,5]{2,1,0:T(1,128)}), s32[8,1,5]{2,1,0:T(1,128)S(1)}, u32[]{:S(2)}, u32[]{:S(2)}) async-start(s32[8,1,5]{2,1,0:T(1,128)} %bitcast), calls=%async_computation | async-start | bytes 8192 | tf_op jit(solution)/shard_map/all_to_all | solution.py:71
  72.9 76.3 %all-gather.2.cloned.1.call-done = bf16[2048,3072]{1,0:T(8,128)(2,1)} async-done(((bf16[2048,768]{1,0:T(8,128)(2,1)}), bf16[2048,3072]{1,0:T(8,128)(2,1)}) %all-gather.2.cloned.1.call-update) | async-done | bytes 12582928 | tf_op jit(solution)/shard_map/all_gather | solution.py:44
  149.2 15.4 %negate_convert_fusion = bf16[3072,768]{1,0:T(8,128)(2,1)} fusion(bf16[2048,3072]{1,0:T(8,128)(2,1)} %all-gather.2.cloned.1.call-done, bf16[2048,768]{1,0:T(8,128)(2,1)} %copy-done), kind=kOutput, calls=%fused_computation.3 | convolution fusion | flops 9668395008 | bytes 20447232 | tf_op jit(solution)/shard_map/dot_general | solution.py:32
  164.6 6.7 %copy.53 = bf16[3072,768]{0,1:T(8,128)(2,1)} copy(bf16[3072,768]{1,0:T(8,128)(2,1)} %negate_convert_fusion) | data formatting | bytes 9437184 | tf_op jit(solution)/shard_map/convert_element_type | solution.py:49
  171.2 9.1 %reshape.124 = bf16[12,256,3,256]{1,0,3,2:T(8,128)(2,1)} reshape(bf16[3072,768]{0,1:T(8,128)(2,1)} %copy.53) | data formatting | bytes 9437184 | tf_op jit(solution)/shard_map/reshape | solution.py:49
  180.4 9.1 %copy.54 = bf16[12,3,256,256]{3,2,1,0:T(8,128)(2,1)} copy(bf16[12,3,256,256]{2,0,3,1:T(8,128)(2,1)} %bitcast.177) | data formatting | bytes 9437184 | tf_op jit(solution)/shard_map/transpose | solution.py:51
  189.5 2.9 pad.9
  192.4 3.1 copy.69
  195.5 3.9 convolution_convert_fusion
  199.4 8.1 %reshape.126 = bf16[8,5,65536]{2,1,0:T(8,128)(2,1)} reshape(bf16[40,65536]{1,0:T(8,128)(2,1)} %convolution_convert_fusion) | data formatting | bytes 10485760 | tf_op jit(solution)/shard_map/reshape | solution.py:66
  207.5 5.6 %all-to-all-start.1 = ((bf16[8,5,65536]{2,1,0:T(8,128)(2,1)}), bf16[8,5,65536]{2,1,0:T(8,128)(2,1)}, u32[]{:S(2)}, u32[]{:S(2)}) async-start(bf16[8,5,65536]{2,1,0:T(8,128)(2,1)} %reshape.126), calls=%async_computation.1 | async-start | bytes 16777216 | tf_op jit(solution)/shard_map/all_to_all | solution.py:70
  213.1 3.2 copy.68
  217.5 179.1 %all-to-all-done.1 = bf16[8,5,65536]{2,1,0:T(8,128)(2,1)} async-done(((bf16[8,5,65536]{2,1,0:T(8,128)(2,1)}), bf16[8,5,65536]{2,1,0:T(8,128)(2,1)}, u32[]{:S(2)}, u32[]{:S(2)}) %all-to-all-start.1) | async-done | bytes 5242912 | tf_op jit(solution)/shard_map/all_to_all | solution.py:70
  396.7 8.2 %reshape.127 = bf16[40,65536]{1,0:T(8,128)(2,1)} reshape(bf16[8,5,65536]{2,1,0:T(8,128)(2,1)} %all-to-all-done.1) | data formatting | bytes 10485760 | tf_op jit(solution)/shard_map/reshape | solution.py:80
  404.8 4.9 %fusion = bf16[16,65536]{1,0:T(8,128)(2,1)S(1)} fusion(f32[16,65536]{1,0:T(8,128)} %bitcast.181, bf16[40,65536]{1,0:T(8,128)(2,1)} %reshape.127, s32[40]{0:T(128)S(1)} %eq.48), kind=kOutput, calls=%fused_computation.2 | convolution fusion | flops 85983872 | bytes 11534496 | tf_op jit(solution)/shard_map/dot_general | solution.py:78
  (92 shorter events, 41.2 us)
Async XLA Ops:
  6.5 142.7 %all-gather.2.cloned.1.call-start = ((), (), s32[]{:S(2)}) async-start(), calls=%async_computation.2 | async-start | bytes 15728640 | tf_op jit(solution)/shard_map/all_gather | solution.py:44
  6.5 8.1 %copy-start.1 = (bf16[1,28,256,256]{3,2,1,0:T(8,128)(2,1)S(1)}, bf16[1,28,256,256]{3,2,1,0:T(8,128)(2,1)}, u32[]{:S(2)}) copy-start(bf16[1,28,256,256]{3,2,1,0:T(8,128)(2,1)} %param.6) | copy-start | bytes 11010052
  8.5 7.2 %copy-start.2 = (bf16[1,2048,768]{2,1,0:T(8,128)(2,1)S(1)}, bf16[1,2048,768]{2,1,0:T(8,128)(2,1)}, u32[]{:S(2)}) copy-start(bf16[1,2048,768]{2,1,0:T(8,128)(2,1)} %param.8) | copy-start | bytes 9437188
  17.2 6.5 %slice-start = ((bf16[1,28,256,256]{3,2,1,0:T(8,128)(2,1)}), bf16[1,2,256,256]{3,2,1,0:T(8,128)(2,1)S(1)}, s32[]{:S(2)}) async-start(bf16[1,28,256,256]{3,2,1,0:T(8,128)(2,1)} %param.6), calls=%async_computation.3 | async-start | bytes 524288 | tf_op jit(solution)/shard_map/slice | solution.py:16
  24.6 8.0 %copy-start.6 = (bf16[1,256,768]{2,1,0:T(8,128)(2,1)S(1)}, bf16[1,256,768]{2,1,0:T(8,128)(2,1)}, u32[]{:S(2)}) copy-start(bf16[1,256,768]{2,1,0:T(8,128)(2,1)} %get-tuple-element.7) | copy-start | bytes 1179652
  35.7 8.4 %copy-start.5 = (bf16[256,768]{1,0:T(8,128)(2,1)S(1)}, bf16[256,768]{1,0:T(8,128)(2,1)}, u32[]{:S(2)}) copy-start(bf16[256,768]{1,0:T(8,128)(2,1)} %get-tuple-element.37) | copy-start | bytes 1179652
  44.1 4.4 %copy-start.17 = (bf16[1,256,768]{1,2,0:T(8,128)(2,1)S(1)}, bf16[1,256,768]{1,2,0:T(8,128)(2,1)}, u32[]{:S(2)}) copy-start(bf16[1,256,768]{1,2,0:T(8,128)(2,1)} %copy.56) | copy-start | bytes 1179652
  44.1 4.4 %copy-start.18 = (bf16[1,2,256,256]{2,3,1,0:T(8,128)(2,1)S(1)}, bf16[1,2,256,256]{2,3,1,0:T(8,128)(2,1)}, u32[]{:S(2)}) copy-start(bf16[1,2,256,256]{2,3,1,0:T(8,128)(2,1)} %copy.57) | copy-start | bytes 786436
  45.5 3.4 copy-start.3
  48.5 2.3 copy-start.15
  48.5 2.3 copy-start.16
  50.9 2.3 copy-start.20
  51.4 3.3 copy-start.10
  51.4 3.3 copy-start.14
  54.7 1.8 copy-start.21
  54.7 2.6 copy-start.9
  54.7 2.6 copy-start.13
  59.0 1.7 copy-start.7
  59.0 1.7 copy-start.11
  61.7 2.5 copy-start.22
  61.7 2.7 copy-start.23
  65.6 141.8 %all-to-all-start = ((s32[8,1,5]{2,1,0:T(1,128)}), s32[8,1,5]{2,1,0:T(1,128)S(1)}, u32[]{:S(2)}, u32[]{:S(2)}) async-start(s32[8,1,5]{2,1,0:T(1,128)} %bitcast), calls=%async_computation | async-start | bytes 8192 | tf_op jit(solution)/shard_map/all_to_all | solution.py:71
  207.5 5.7 %copy-start.4 = (bf16[1,16,256,256]{3,2,1,0:T(8,128)(2,1)S(1)}, bf16[1,16,256,256]{3,2,1,0:T(8,128)(2,1)}, u32[]{:S(2)}) copy-start(bf16[1,16,256,256]{3,2,1,0:T(8,128)(2,1)} %param.11) | copy-start | bytes 6291460
  207.5 189.2 %all-to-all-start.1 = ((bf16[8,5,65536]{2,1,0:T(8,128)(2,1)}), bf16[8,5,65536]{2,1,0:T(8,128)(2,1)}, u32[]{:S(2)}, u32[]{:S(2)}) async-start(bf16[8,5,65536]{2,1,0:T(8,128)(2,1)} %reshape.126), calls=%async_computation.1 | async-start | bytes 16777216 | tf_op jit(solution)/shard_map/all_to_all | solution.py:70
  (4 other events, 6.4 us)
Sparse Core Ops, SparseCore 0:
  64.3 84.8 all-gather.1
where the time goes:
time: 420 us; the launch traced here: 418 us
  waiting for transfers between devices  255 us (61%)
  local copies, waits for them, and re-layouts  93.2 us (22%)
  matrix products  42.1 us (10%)
  between operations  13.7 us (3%)
  starting transfers between devices  12.9 us (3%)
    all_to_all x1, waiting for transfers between devices, shards(): lax.all_to_all(outgoing, 'sub', split_axis=0, concat_axis=0, tiled=True)  179 us
    all_gather x1, waiting for transfers between devices, shards(): lax.all_gather(own_solved, 'tile', axis=1, tiled=True)  76.3 us
    unnamed x66, local copies, waits for them, and re-layouts  39.9 us
    dot_general x1, matrix products, inner_rows(): lax.dot_general(left_part, right_part, (((0,), (0,)), ((), ())), preferre...  15.4 us
    dot_general x8, matrix products, solve(): jnp.dot(inverse[row_panel], target, precision=lax.Precision.HIGHEST, pref...  12.6 us
    reshape x1, local copies, waits for them, and re-layouts, shards(): (-schur_cols).astype(jnp.bfloat16)  9.15 us
    transpose x1, local copies, waits for them, and re-layouts, shards(): contrib.transpose(0, 2, 1, 3).reshape(tile_count, panel_width * panel_width)  9.08 us
    slice x7, local copies, waits for them, and re-layouts, solve(): blocks = lower_blocks[block_start:block_start + row_panel]  9.07 us
  transfers between devices with their start and end apart: 3, of which 2 were waited for; matrix products, arithmetic and copies ran while one was open for 15% of the time, Pallas kernels for 0%

commit v1 on v0

v1 whole, which is shorter than its diff:
```python
import functools

import jax
import jax.numpy as jnp
from jax import lax
from jax.experimental import pallas as pl
from jax.experimental.pallas import tpu as pltpu
from jax.sharding import PartitionSpec as P

MESH = pl.DeviceIdType.MESH
F32 = jnp.float32
BF16 = jnp.bfloat16


def exchange_kernel(
    dims,
    meta_sm,
    meta_any,
    coupling_hbm,
    inverse_hbm,
    cols_hbm,
    incoming,
    metas,
    labels,
    coupling,
    inverse,
    cols,
    target,
    held,
    total,
    packed,
    table,
    meta_all,
    load_sem,
    own_send,
    own_recv,
    relay_send,
    relay_recv,
    out_send,
    out_recv,
    meta_send,
    meta_recv,
    local_sem,
):
    n_sub, n_tile, panels, width, col_tiles, tile_count, capacity, slots = dims
    me = lax.axis_index("sub")
    col = lax.axis_index("tile")
    half_tile = n_tile // 2
    partner = col + 1 - 2 * (col % 2)
    across = (col + half_tile) % n_tile
    corner = (partner + half_tile) % n_tile
    places = (col, partner, across, corner)
    half = n_sub // 2
    side = me // half
    within = me % half

    def far_peer(j):
        return ((side + 1) % 2) * half + (within + j) % half

    def near_peer(j):
        return side * half + (within + j) % half

    loads = [
        pltpu.make_async_copy(cols_hbm.at[0], cols.at[0], load_sem.at[0]),
        pltpu.make_async_copy(inverse_hbm.at[0], inverse.at[0], load_sem.at[1]),
        pltpu.make_async_copy(coupling_hbm, coupling, load_sem.at[2]),
        pltpu.make_async_copy(
            inverse_hbm.at[pl.ds(1, panels - 1)], inverse.at[pl.ds(1, panels - 1)], load_sem.at[3]
        ),
        pltpu.make_async_copy(
            cols_hbm.at[pl.ds(1, panels - 1)], cols.at[pl.ds(1, panels - 1)], load_sem.at[4]
        ),
    ]
    for load in loads:
        load.start()

    barrier = pltpu.get_barrier_semaphore()
    for place in (partner, across):
        pl.semaphore_signal(barrier, inc=1, device_id={"tile": place}, device_id_type=MESH)

    @pl.loop(1, n_sub)
    def _(j):
        pl.semaphore_signal(
            barrier, inc=1, device_id={"sub": (me + j) % n_sub}, device_id_type=MESH
        )

    def solve_panel(k):
        target[...] = cols[k].astype(F32)
        start = k * (k - 1) // 2
        for m in range(k):
            target[...] -= jnp.dot(coupling[start + m], held[m], preferred_element_type=F32)
        inv = inverse[k]
        inv_high = inv.astype(BF16)
        inv_low = (inv - inv_high.astype(F32)).astype(BF16)
        value = target[...]
        high = value.astype(BF16)
        low = (value - high.astype(F32)).astype(BF16)
        answer = jnp.dot(inv_high, low, preferred_element_type=F32)
        answer += jnp.dot(inv_low, high, preferred_element_type=F32)
        answer += jnp.dot(inv_high, high, preferred_element_type=F32)
        held[k] = answer.astype(BF16)

    def own_copy(k, way):
        return pltpu.make_async_remote_copy(
            src_ref=held.at[k],
            dst_ref=held.at[(way + 1) * panels + k],
            send_sem=own_send.at[way, k],
            recv_sem=own_recv.at[way, k],
            device_id={"tile": (partner, across)[way]},
            device_id_type=MESH,
        )

    def relay_copy(k):
        return pltpu.make_async_remote_copy(
            src_ref=held.at[2 * panels + k],
            dst_ref=held.at[3 * panels + k],
            send_sem=relay_send.at[k],
            recv_sem=relay_recv.at[k],
            device_id={"tile": partner},
            device_id_type=MESH,
        )

    def out_copy(peer, source):
        return pltpu.make_async_remote_copy(
            src_ref=packed.at[peer],
            dst_ref=incoming.at[source],
            send_sem=out_send.at[peer],
            recv_sem=out_recv.at[source],
            device_id={"sub": peer},
            device_id_type=MESH,
        )

    def meta_copy(peer, source):
        return pltpu.make_async_remote_copy(
            src_ref=meta_any,
            dst_ref=metas.at[source],
            send_sem=meta_send.at[peer],
            recv_sem=meta_recv.at[source],
            device_id={"sub": peer},
            device_id_type=MESH,
        )

    loads[0].wait()
    loads[1].wait()
    solve_panel(0)
    pl.semaphore_wait(barrier, n_sub + 1)
    own_copy(0, 1).start()
    own_copy(0, 0).start()
    for load in loads[2:]:
        load.wait()
    for k in range(1, panels):
        solve_panel(k)
        own_copy(k, 1).start()
        own_copy(k, 0).start()

    @pl.loop(1, n_sub)
    def _(j):
        meta_copy((me + j) % n_sub, me).start()

    per_place = col_tiles * col_tiles

    def gram(u, k, first=False):
        right = held[k]
        for i in range(col_tiles):
            left = held[u * panels + k, :, i * width : (i + 1) * width]
            product = lax.dot_general(
                left, right, (((0,), (0,)), ((), ())), preferred_element_type=F32
            )
            for j in range(col_tiles):
                piece = product[:, j * width : (j + 1) * width]
                at = places[u] * per_place + i * col_tiles + j
                if first:
                    total[at] = piece
                else:
                    total[at] += piece

    def pick(read, low, default, value_of, store):
        def body(i, carry):
            count, chosen = carry
            value = read(i)
            hit = (value >= low) & (value < low + slots)
            new = value_of(i, value)
            chosen = tuple(
                jnp.where(hit & (count == r), new, c) for r, c in enumerate(chosen)
            )
            return count + jnp.where(hit, 1, 0), chosen

        start = (jnp.int32(0), tuple(jnp.int32(default) for _ in range(capacity)))
        _, chosen = lax.fori_loop(0, tile_count, body, start)
        for r, c in enumerate(chosen):
            store(r, c)

    @pl.loop(0, n_sub)
    def _(d):
        def store(r, c):
            table[d * capacity + r] = c

        pick(lambda i: meta_sm[0, i], d * slots, 0, lambda i, v: i, store)

    gram(0, 0, first=True)

    @pl.loop(1, panels)
    def _(k):
        gram(0, k)

    own_copy(0, 0).wait_recv()
    gram(1, 0, first=True)

    @pl.loop(1, panels)
    def _(k):
        own_copy(k, 0).wait_recv()
        gram(1, k)

    def remote_step(k, first):
        own_copy(k, 1).wait_recv()
        relay_copy(k).start()
        gram(2, k, first)
        relay_copy(k).wait_recv()
        gram(3, k, first)

    remote_step(0, True)

    @pl.loop(1, panels)
    def _(k):
        remote_step(k, False)

    def pack(d):
        for r in range(capacity):
            packed[d, r] = (-total[table[d * capacity + r]]).astype(BF16)

    @pl.loop(0, half)
    def _(j):
        pack(far_peer(j))
        out_copy(far_peer(j), me).start()

    @pl.loop(1, half)
    def _(j):
        pack(near_peer(j))
        out_copy(near_peer(j), me).start()

    pack(me)
    keep = pltpu.make_async_copy(packed.at[me], incoming.at[me], local_sem.at[0])
    keep.start()

    own_meta = pltpu.make_async_copy(meta_any, meta_all.at[me], local_sem.at[1])
    own_meta.start()

    @pl.loop(1, n_sub)
    def _(j):
        source = (me + j) % n_sub
        meta_copy(source, source).wait_recv()
        fetch = pltpu.make_async_copy(metas.at[source], meta_all.at[source], local_sem.at[2])
        fetch.start()
        fetch.wait()

    own_meta.wait()

    @pl.loop(0, n_sub)
    def _(s):
        def store(r, c):
            labels[s * capacity + r] = c

        pick(
            lambda i: meta_all[s, 0, i], me * slots, slots, lambda i, v: v - me * slots, store
        )

    @pl.loop(0, panels)
    def _(k):
        own_copy(k, 0).wait_send()
        own_copy(k, 1).wait_send()
        relay_copy(k).wait_send()

    @pl.loop(1, n_sub)
    def _(j):
        source = (me + j) % n_sub
        meta_copy(source, source).wait_send()
        out_copy(source, source).wait_send()
        out_copy(source, source).wait_recv()

    keep.wait()


def add_kernel(slots, capacity, labels, incoming, base, result, total):
    step = pl.program_id(0)

    @pl.when(step == 0)
    def _():
        total[pl.ds(0, slots)] = base[...].astype(F32)

    for r in range(capacity):
        total[labels[step * capacity + r]] += incoming[0, r].astype(F32)

    @pl.when(step == pl.num_programs(0) - 1)
    def _():
        result[...] = total[pl.ds(0, slots)].astype(BF16)


def shards(coupling, panel_inv, a_ib, owner, slot, base):
    lower_blocks = coupling[0]
    inverse = panel_inv[0]
    panels, width = inverse.shape[:2]
    col_count = a_ib.shape[2]
    right_cols = a_ib[0].reshape(panels, width, col_count)
    n_sub = lax.axis_size("sub")
    n_tile = lax.axis_size("tile")
    assert n_tile == 4 and n_sub % 2 == 0
    col_tiles = col_count // width
    tile_count = owner.shape[1] * owner.shape[2]
    assert owner.shape[1] == n_tile * col_tiles
    capacity = (tile_count + n_sub - 1) // n_sub
    slots = base.shape[1]
    room = (tile_count + 127) // 128 * 128
    meta = (owner[0] * slots + slot[0]).reshape(1, tile_count)
    meta = jnp.pad(meta, ((0, 0), (0, room - tile_count)))
    dims = (n_sub, n_tile, panels, width, col_tiles, tile_count, capacity, slots)
    any_spec = pl.BlockSpec(memory_space=pl.ANY)
    smem_spec = pl.BlockSpec(memory_space=pltpu.SMEM)
    dma = pltpu.SemaphoreType.DMA
    incoming, _, labels = pl.pallas_call(
        functools.partial(exchange_kernel, dims),
        out_shape=(
            jax.ShapeDtypeStruct((n_sub, capacity, width, width), BF16),
            jax.ShapeDtypeStruct((n_sub, 1, room), jnp.int32),
            jax.ShapeDtypeStruct((n_sub * capacity,), jnp.int32),
        ),
        in_specs=[smem_spec, any_spec, any_spec, any_spec, any_spec],
        out_specs=(any_spec, any_spec, smem_spec),
        scratch_shapes=[
            pltpu.VMEM(lower_blocks.shape, BF16),
            pltpu.VMEM(inverse.shape, F32),
            pltpu.VMEM(right_cols.shape, BF16),
            pltpu.VMEM((width, col_count), F32),
            pltpu.VMEM((n_tile * panels, width, col_count), BF16),
            pltpu.VMEM((tile_count, width, width), F32),
            pltpu.VMEM((n_sub, capacity, width, width), BF16),
            pltpu.SMEM((n_sub * capacity,), jnp.int32),
            pltpu.SMEM((n_sub, 1, room), jnp.int32),
            dma((5,)),
            dma((2, panels)),
            dma((2, panels)),
            dma((panels,)),
            dma((panels,)),
            dma((n_sub,)),
            dma((n_sub,)),
            dma((n_sub,)),
            dma((n_sub,)),
            dma((3,)),
        ],
        compiler_params=pltpu.CompilerParams(
            collective_id=0, has_side_effects=True, vmem_limit_bytes=60 * 1024 * 1024
        ),
    )(meta, meta, lower_blocks, inverse, right_cols)

    whole_block = pl.BlockSpec((slots, width, width), lambda s: (0, 0, 0))
    result = pl.pallas_call(
        functools.partial(add_kernel, slots, capacity),
        grid=(n_sub,),
        out_shape=jax.ShapeDtypeStruct((slots, width, width), BF16),
        in_specs=[
            smem_spec,
            pl.BlockSpec((1, capacity, width, width), lambda s: (s, 0, 0, 0)),
            whole_block,
        ],
        out_specs=whole_block,
        scratch_shapes=[pltpu.VMEM((slots + 1, width, width), F32)],
        compiler_params=pltpu.CompilerParams(vmem_limit_bytes=32 * 1024 * 1024),
    )(labels, incoming, base[0])
    return result[None]


def solution(mesh):
    placed = (
        P("sub", None, None, None),
        P("sub", None, None, None),
        P("sub", None, "tile"),
        P("sub", None, "tile"),
        P("sub", None, "tile"),
        P("sub", "tile", None, None),
    )
    return jax.shard_map(
        shards, mesh=mesh, in_specs=placed, out_specs=P("sub", "tile", None, None), check_vma=False
    )
```

time: 420 us -> 202 us (0.48)
  waiting for transfers between devices: 255 us -> 0 us
  Pallas kernels: 0 us -> 198 us
  local copies, waits for them, and re-layouts: 93.2 us -> 3.79 us
  matrix products: 42.1 us -> 0 us
  between operations: 13.7 us -> 0.03 us
  starting transfers between devices: 12.9 us -> 0 us
    pallas_call x0 -> x2, Pallas kernels: none -> 198 us  [the longest x1 194 us: shards(): pl.pallas_call(functools.partial(exchange_kernel, dims), out_shape=(jax.S...]
    all_to_all x2 -> x0, waiting for transfers between devices: 179 us -> none  [the longest x1 179 us: shards(): lax.all_to_all(outgoing, 'sub', split_axis=0, concat_axis=0, tiled=True)]
    all_gather x1 -> x0, waiting for transfers between devices: 76.3 us -> none  [shards(): lax.all_gather(own_solved, 'tile', axis=1, tiled=True)]
    dot_general x18 -> x0, matrix products: 42.1 us -> none  [the longest x1 15.4 us: inner_rows(): lax.dot_general(left_part, right_part, (((0,), (0,)), ((), ())), preferre...]
    unnamed x66 -> x6, local copies, waits for them, and re-layouts: 39.9 us -> 3.09 us
    reshape x3 -> x0, local copies, waits for them, and re-layouts: 25.4 us -> none  [the longest x1 9.15 us: shards(): (-schur_cols).astype(jnp.bfloat16)]
    all_to_all x2 -> x0, starting transfers between devices: 12.9 us -> none  [the longest x1 7.3 us: shards(): lax.all_to_all(labels, 'sub', split_axis=0, concat_axis=0, tiled=True)]
    slice x8 -> x0, local copies, waits for them, and re-layouts: 10.6 us -> none  [the longest x7 9.07 us: solve(): blocks = lower_blocks[block_start:block_start + row_panel]]
  transfers between devices with their start and end apart: 3 -> 0, of which waited for: 2 -> 0; matrix products, arithmetic and copies ran while one was open for 15% -> 0% of each run, Pallas kernels for 0% -> 0%
where the time goes in v1:
time: 202 us
  Pallas kernels  198 us (98%)
  local copies, waits for them, and re-layouts  3.79 us (2%)
    pallas_call x1, Pallas kernels, shards(): pl.pallas_call(functools.partial(exchange_kernel, dims), out_shape=(jax.S...  194 us

profile of v1, /device:TPU:0, one launch (start us, length us, event | category | flops | bytes accessed | tf_op | source)
XLA Modules:
  0.0 202.1 jit_solution(15653830999405506191)
XLA Ops:
  0.0 0.7 multiply_add_fusion
  0.7 0.1 copy.8
  0.8 0.1 add.16
  0.9 0.5 pad.4.meta_sm.meta_any
  1.4 0.0 copy-start.1
  1.4 194.1 %shard_map.64 = (bf16[8,5,256,256]{3,2,1,0:T(8,128)(2,1)}, s32[8,1,128]{2,1,0:T(1,128)}, s32[40]{0:T(128)}) custom-call(s32[1,128]{1,0:T(1,128)} %pad.4.meta_sm.meta_any, s32[1,128]{1,0:T(1,128)} %pad.4.meta_sm.meta_any, bf16[28,256,256]{2,1,0:T(8,128)(2,1)} %bitcast.6, f32[8,256,256]{2,1,0:T(8,128)} %bitcast.8, bf16[8,256,768]{2,1,0:T(8,128)(2,1)} %bitcast.7), custom_call_target="tpu_custom_call" | custom-call | tf_op jit(solution)/shard_map/pallas_call | solution.py:319
  195.5 0.0 copy-done.1
  195.5 0.0 copy-start
  195.5 2.5 %copy-done = bf16[8,5,256,256]{3,2,1,0:T(8,128)(2,1)S(1)} copy-done((bf16[8,5,256,256]{3,2,1,0:T(8,128)(2,1)S(1)}, bf16[8,5,256,256]{3,2,1,0:T(8,128)(2,1)}, u32[]{:S(2)}) %copy-start) | copy-done | bytes 5242904
  198.0 0.0 copy-start.2
  198.0 0.6 copy-done.2
  198.6 3.5 %shard_map.65 = bf16[16,256,256]{2,1,0:T(8,128)(2,1)} custom-call(s32[40]{0:T(128)S(1)} %copy-done.2, bf16[8,5,256,256]{3,2,1,0:T(8,128)(2,1)S(1)} %copy-done, bf16[16,256,256]{2,1,0:T(8,128)(2,1)S(1)} %bitcast.5), custom_call_target="tpu_custom_call" | custom-call | tf_op jit(solution)/shard_map/pallas_call | solution.py:355
Async XLA Ops:
  1.4 194.1 %copy-start.1 = (bf16[1,16,256,256]{3,2,1,0:T(8,128)(2,1)S(1)}, bf16[1,16,256,256]{3,2,1,0:T(8,128)(2,1)}, u32[]{:S(2)}) copy-start(bf16[1,16,256,256]{3,2,1,0:T(8,128)(2,1)} %param.11) | copy-start | bytes 6291460
  195.5 2.5 %copy-start = (bf16[8,5,256,256]{3,2,1,0:T(8,128)(2,1)S(1)}, bf16[8,5,256,256]{3,2,1,0:T(8,128)(2,1)}, u32[]{:S(2)}) copy-start(bf16[8,5,256,256]{3,2,1,0:T(8,128)(2,1)} %get-tuple-element.8.incoming) | copy-start | bytes 15728644
  198.0 0.6 copy-start.2

commit v2 on v1

--- a/solution.py
+++ b/solution.py
@@ -363,7 +363,7 @@
         ],
         out_specs=whole_block,
         scratch_shapes=[pltpu.VMEM((slots + 1, width, width), F32)],
-        compiler_params=pltpu.CompilerParams(vmem_limit_bytes=32 * 1024 * 1024),
+        compiler_params=pltpu.CompilerParams(vmem_limit_bytes=62 * 1024 * 1024),
     )(labels, incoming, base[0])
     return result[None]
 

time: 202 us -> 203 us (level)
  Pallas kernels: 198 us -> 202 us
  local copies, waits for them, and re-layouts: 3.79 us -> 0.7 us
    pallas_call x1, Pallas kernels: 3.47 us -> 7.78 us  [shards(): pl.pallas_call(functools.partial(add_kernel, slots, capacity), grid=(n_su...]
    unnamed x6 -> x0, local copies, waits for them, and re-layouts: 3.09 us -> none
where the time goes in v2:
time: 203 us
  Pallas kernels  202 us (100%)
    pallas_call x1, Pallas kernels, shards(): pl.pallas_call(functools.partial(exchange_kernel, dims), out_shape=(jax.S...  194 us
    pallas_call x1, Pallas kernels, shards(): pl.pallas_call(functools.partial(add_kernel, slots, capacity), grid=(n_su...  7.78 us

profile of v2, /device:TPU:0, one launch (start us, length us, event | category | flops | bytes accessed | tf_op | source)
XLA Modules:
  0.0 203.1 jit_solution(3660533986090037189)
XLA Ops:
  0.0 0.7 multiply_add_fusion
  0.7 0.1 copy.8
  0.8 0.1 add.16
  0.9 0.5 pad.4.meta_sm.meta_any
  1.4 193.9 %shard_map.64 = (bf16[8,5,256,256]{3,2,1,0:T(8,128)(2,1)}, s32[8,1,128]{2,1,0:T(1,128)}, s32[40]{0:T(128)}) custom-call(s32[1,128]{1,0:T(1,128)} %pad.4.meta_sm.meta_any, s32[1,128]{1,0:T(1,128)} %pad.4.meta_sm.meta_any, bf16[28,256,256]{2,1,0:T(8,128)(2,1)} %bitcast.5, f32[8,256,256]{2,1,0:T(8,128)} %bitcast.7, bf16[8,256,768]{2,1,0:T(8,128)(2,1)} %bitcast.6), custom_call_target="tpu_custom_call" | custom-call | tf_op jit(solution)/shard_map/pallas_call | solution.py:319
  195.4 7.8 %shard_map.65 = bf16[16,256,256]{2,1,0:T(8,128)(2,1)} custom-call(s32[40]{0:T(128)} %get-tuple-element.7.labels, bf16[8,5,256,256]{3,2,1,0:T(8,128)(2,1)} %get-tuple-element.8.incoming, bf16[16,256,256]{2,1,0:T(8,128)(2,1)} %bitcast.8), custom_call_target="tpu_custom_call" | custom-call | tf_op jit(solution)/shard_map/pallas_call | solution.py:355
